TPU v7x, 256 devices: a whole 4x4x8 slice. The times are simulated.
256 devices in a mesh: seq: 32 (over z, y), batch: 8 (over x, core).
Axes of the slice: x: 4, y: 4, z: 8, core: 2. Of those that a mesh axis runs over, the one named last changes fastest.
Arguments:
- inputs: bfloat16 [65536, 4096], P(('batch', 'seq')), parts along dimension 0, may hold values from -6 to 6
- recur_weight: bfloat16 [16, 256, 256], replicated, may hold values from -0.375 to 0.375
- input_weight: bfloat16 [16, 256, 256], replicated, may hold values from -0.375 to 0.375
- recur_bias: float32 [4096], replicated, may hold values from -4 to 4
- input_bias: float32 [4096], replicated, may hold values from -4 to 4
- decay_rate: float32 [4096], replicated, may hold values from 1.2207031e-06 to 0.02
- kv_weight: bfloat16 [4096, 512], replicated, may hold values from -61 to 61
Outputs:
- attended: bfloat16 [65536, 4096], P(('batch', 'seq')), parts along dimension 0
There are 8 independent parts, one for each index of `batch`. A program takes and returns all parts, laid end to end along the dimension named above; an argument that names none is the same for every part. Nothing has to cross between parts.
All inputs are finite; a program needn't handle non-finite values.
Results may differ from a plain program's by a relative error of at most 0.03.
Values may be sent and summed in bfloat16 or wider, within the bound.
A program may use at most 128 MiB of HBM per device.

v0:
```python
import math

import jax
import jax.numpy as jnp
from jax import lax
from jax.experimental import pallas as pl
from jax.experimental.pallas import tpu as pltpu
from jax.sharding import PartitionSpec as P

TOK = 256
D = 4096
HD = 256
HEADS = 16
ROWS = 8
COLS = 4
CHUNKS = 4
PER = HEADS // CHUNKS
LOG2E = math.log2(math.e)
SCALE2 = (HD ** -0.5) * LOG2E
NEG = -1e30
F32 = jnp.float32
BF16 = jnp.bfloat16
MESH = pl.DeviceIdType.MESH

STEPS = ((4,), (1, 3), (8, 5), (2, 7), (6,))
PLACE = {0: 0}
for _step in STEPS:
    for _o in _step:
        PLACE[_o] = len(PLACE)


def token_of(row):
    return (row % 8) * 32 + row // 8


def permutation(transposed):
    rows = lax.broadcasted_iota(jnp.int32, (TOK, TOK), 1 if transposed else 0)
    toks = lax.broadcasted_iota(jnp.int32, (TOK, TOK), 0 if transposed else 1)
    return (token_of(rows) == toks).astype(F32).astype(BF16)


def row_distance(o, y):
    return (o - y + COLS - 1) // COLS


class Halo:
    def __init__(self, kv, send, recv, z, y):
        self.kv, self.send, self.recv, self.z, self.y = kv, send, recv, z, y
        self.count = [0] * COLS
        self.waited = [set() for _ in range(COLS)]
        self.started = [[] for _ in range(COLS)]

    def half(self, o, part):
        return self.kv.at[PLACE[o], pl.ds(part * HD, HD)]

    def copy(self, index, src, dst, part, dz, dst_y):
        return pltpu.make_async_remote_copy(
            src_ref=self.half(src, part),
            dst_ref=self.half(dst, part),
            send_sem=self.send.at[index],
            recv_sem=self.recv.at[PLACE[dst], part],
            device_id={"seq": (self.z + dz) * COLS + dst_y},
            device_id_type=MESH,
        )

    def start(self, yy, src, part, dz, dst_y):
        dst = src + dz * COLS + dst_y - yy
        low = row_distance(src, yy)
        high = ROWS - 2 if dz else ROWS - 1
        index = self.count[yy]
        self.count[yy] += 1
        args = (index, src, dst, part, dz, dst_y)

        @pl.when((self.z >= low) & (self.z <= high))
        def _():
            self.copy(*args).start()

        self.started[yy].append((low, high, args))

    def arrive(self, yy, o, part):
        if (o, part) in self.waited[yy]:
            return
        self.waited[yy].add((o, part))

        @pl.when(self.z >= row_distance(o, yy))
        def _():
            pltpu.make_async_remote_copy(
                src_ref=self.half(o, part),
                dst_ref=self.half(o, part),
                send_sem=self.send.at[0],
                recv_sem=self.recv.at[PLACE[o], part],
                device_id={"seq": self.z * COLS + self.y},
                device_id_type=MESH,
            ).wait_recv()

    def each(self, fn):
        for yy in range(COLS):
            @pl.when(self.y == yy)
            def _():
                fn(yy)

    def own(self, yy):
        for part in (0, 1):
            self.start(yy, 0, part, 1, yy)
            if yy < COLS - 1:
                self.start(yy, 0, part, 0, yy + 1)
            if yy == 0:
                self.start(yy, 0, part, 0, COLS - 1)

    def first_row(self, yy):
        for part in (0, 1):
            self.arrive(yy, 4, part)
            self.start(yy, 4, part, 1, yy)
            self.start(yy, 4, part, 0, (yy + 1) % COLS)
            self.start(yy, 4, part, 0, (yy - 1) % COLS)
            if yy == 1 and part == 0:
                self.arrive(yy, 1, 0)
                self.start(yy, 1, 0, 0, 2)
            if yy == 2:
                self.arrive(yy, 1, part)
                self.start(yy, 1, part, 0, 3)
            if yy == 3 and part == 1:
                self.arrive(yy, 3, 1)
                self.start(yy, 3, 1, 0, 2)

    def second_row(self, yy):
        left, right = (yy - 1) % COLS, (yy + 1) % COLS
        from_left, from_right = 4 + yy - left, 4 + yy - right
        self.arrive(yy, from_left, 0)
        self.start(yy, from_left, 0, 0, right)
        for part in (0, 1):
            self.arrive(yy, 8, part)
            if yy >= 1:
                self.start(yy, 8, part, 0, yy - 1)
            if yy == COLS - 1:
                self.start(yy, 8, part, 0, 0)
        self.arrive(yy, from_right, 1)
        self.start(yy, from_right, 1, 0, left)

    def last_row(self, yy):
        if yy == 0:
            self.arrive(yy, 5, 1)
            self.start(yy, 5, 1, 0, 1)
        if yy == 1:
            for part in (0, 1):
                self.arrive(yy, 7, part)
                self.start(yy, 7, part, 0, 0)
        if yy == 2:
            self.arrive(yy, 7, 0)
            self.start(yy, 7, 0, 0, 1)

    def need(self, step):
        def fn(yy):
            for o in step:
                for part in (0, 1):
                    self.arrive(yy, o, part)

        self.each(fn)

    def drain(self):
        def fn(yy):
            for low, high, args in self.started[yy]:
                @pl.when((self.z >= low) & (self.z <= high))
                def _(args=args):
                    self.copy(*args).wait_send()

        self.each(fn)


def kernel(
    x_hbm, wr_hbm, wi_hbm, br, bi, rate, wkv_hbm, out_hbm,
    x, wr, wi, wkv, perm, xp_a, lr_a, li_a, xp_b, lr_b, li_b, loc, cum, segc, segp,
    rowtot, rowpre, coltot, carry, hid, kvacc, kv, bias0, bias8,
    m, l, acc, s_a, s_b, p_a, p_b, al_a, al_b, out,
    load_sem, row_send, row_recv, col_send, col_recv, halo_send, halo_recv, out_sem,
):
    me = lax.axis_index("seq")
    z, y = me // COLS, me % COLS

    loads = []
    for c in range(CHUNKS):
        cols, blocks = pl.ds(c * PER * HD, PER * HD), pl.ds(c * PER, PER)
        loads.append([
            pltpu.make_async_copy(x_hbm.at[:, cols], x.at[:, cols], load_sem.at[3 * c]),
            pltpu.make_async_copy(wr_hbm.at[blocks], wr.at[blocks], load_sem.at[3 * c + 1]),
            pltpu.make_async_copy(wi_hbm.at[blocks], wi.at[blocks], load_sem.at[3 * c + 2]),
        ])
    load_kv = pltpu.make_async_copy(wkv_hbm, wkv, load_sem.at[3 * CHUNKS])
    for group in loads:
        for load in group:
            load.start()
    load_kv.start()

    barrier = pltpu.get_barrier_semaphore()
    for k in range(1, COLS):
        pl.semaphore_signal(
            barrier, inc=1, device_id={"seq": z * COLS + (y + k) % COLS}, device_id_type=MESH
        )
    for k in range(1, ROWS):
        pl.semaphore_signal(
            barrier, inc=1, device_id={"seq": ((z + k) % ROWS) * COLS + y}, device_id_type=MESH
        )

    perm[...] = permutation(False)
    kt = token_of(lax.broadcasted_iota(jnp.int32, (TOK, TOK), 0))
    qt = token_of(lax.broadcasted_iota(jnp.int32, (TOK, TOK), 1))
    bias0[...] = jnp.where(kt <= qt, 0.0, NEG)
    bias8[...] = jnp.where(kt <= qt, NEG, 0.0)

    def lanes(b):
        return pl.ds(pl.multiple_of(b * HD, HD), HD)

    def gates(b, xp_ref, lr_ref, li_ref):
        xp = jnp.dot(perm[...], x[:, lanes(b)], preferred_element_type=F32)
        xb = xp.astype(BF16)
        xp_ref[...] = xp
        lr_ref[...] = jnp.dot(xb, wr[b], preferred_element_type=F32)
        li_ref[...] = jnp.dot(xb, wi[b], preferred_element_type=F32)

    def scan(b, c, xp_ref, lr_ref, li_ref):
        half_r, half_i = br[:, lanes(b)] * 0.5, bi[:, lanes(b)] * 0.5
        coef = rate[:, lanes(b)] * (-4.0 * LOG2E)
        for j in range(32):
            rows = slice(8 * j, 8 * j + 8)
            tr = jnp.tanh(lr_ref[rows] * 0.5 + half_r)
            ti = jnp.tanh(li_ref[rows] * 0.5 + half_i)
            a = jnp.exp2(tr * coef + coef)
            v = jnp.maximum(1.0 - a * a, 1e-37)
            drive = (v * lax.rsqrt(v)) * ((ti * 0.5 + 0.5) * xp_ref[rows])
            if j == 0:
                h, prod = drive, a
            else:
                h, prod = a * h + drive, prod * a
            loc[b, rows] = h
            cum[b, rows] = prod
        start = jnp.zeros((1, HD), F32)
        gain = jnp.ones((1, HD), F32)
        starts, gains = [], []
        for s in range(8):
            starts.append(start)
            gains.append(gain)
            start = prod[s : s + 1] * start + h[s : s + 1]
            gain = gain * prod[s : s + 1]
        segc[b] = jnp.concatenate(starts, axis=0)
        segp[b] = jnp.concatenate(gains, axis=0)
        rowtot[c, y, 0, b - c * PER] = gain
        rowtot[c, y, 1, b - c * PER] = start

    def row_copy(c, k):
        return pltpu.make_async_remote_copy(
            src_ref=rowtot.at[c, y], dst_ref=rowtot.at[c, y],
            send_sem=row_send.at[c, k - 1], recv_sem=row_recv.at[c, y],
            device_id={"seq": z * COLS + (y + k) % COLS}, device_id_type=MESH,
        )

    def row_arrival(c, src):
        return pltpu.make_async_remote_copy(
            src_ref=rowtot.at[c, src], dst_ref=rowtot.at[c, src],
            send_sem=row_send.at[c, 0], recv_sem=row_recv.at[c, src],
            device_id={"seq": me}, device_id_type=MESH,
        )

    def col_copy(c, to):
        return pltpu.make_async_remote_copy(
            src_ref=coltot.at[c, z], dst_ref=coltot.at[c, z],
            send_sem=col_send.at[c, to], recv_sem=col_recv.at[c, z],
            device_id={"seq": to * COLS + y}, device_id_type=MESH,
        )

    def col_arrival(c, src):
        return pltpu.make_async_remote_copy(
            src_ref=coltot.at[c, src], dst_ref=coltot.at[c, src],
            send_sem=col_send.at[c, 0], recv_sem=col_recv.at[c, src],
            device_id={"seq": me}, device_id_type=MESH,
        )

    def send_row(c):
        for k in range(1, COLS):
            row_copy(c, k).start()

    def row_totals(c):
        for k in range(1, COLS):
            row_arrival(c, (y + k) % COLS).wait_recv()
        prod, state = rowtot[c, 0, 0], rowtot[c, 0, 1]
        before_p, before_s = jnp.ones_like(prod), jnp.zeros_like(state)
        for s in range(1, COLS):
            here = s <= y
            before_p = jnp.where(here, prod, before_p)
            before_s = jnp.where(here, state, before_s)
            prod, state = prod * rowtot[c, s, 0], rowtot[c, s, 0] * state + rowtot[c, s, 1]
        rowpre[c, 0] = before_p
        rowpre[c, 1] = before_s
        coltot[c, z, 0] = prod
        coltot[c, z, 1] = state
        for to in range(1, ROWS):
            @pl.when(to > z)
            def _():
                col_copy(c, to).start()

    def hidden(c):
        carry[...] = jnp.zeros(carry.shape, F32)
        for src in range(ROWS - 1):
            @pl.when(src < z)
            def _():
                col_arrival(c, src).wait_recv()
                carry[...] = coltot[c, src, 0] * carry[...] + coltot[c, src, 1]
        carry[...] = rowpre[c, 0] * carry[...] + rowpre[c, 1]
        total = None
        for i in range(PER):
            b = c * PER + i
            g = segc[b] + segp[b] * carry[i]
            value = loc[b].reshape(32, 8, HD) + cum[b].reshape(32, 8, HD) * g[None]
            value = value.reshape(TOK, HD).astype(BF16)
            hid[b] = value
            part = jnp.dot(value, wkv[b], preferred_element_type=F32)
            total = part if total is None else total + part
        if c == 0:
            kvacc[...] = total
        else:
            kvacc[...] += total

    for load in loads[0]:
        load.wait()
    gates(0, xp_a, lr_a, li_a)
    for c in range(CHUNKS):
        if c + 1 < CHUNKS:
            for load in loads[c + 1]:
                load.wait()

        def pair(i, _, c=c):
            b = c * PER + 2 * i
            gates(b + 1, xp_b, lr_b, li_b)
            scan(b, c, xp_a, lr_a, li_a)
            gates(jnp.minimum(b + 2, HEADS - 1), xp_a, lr_a, li_a)
            scan(b + 1, c, xp_b, lr_b, li_b)
            return 0

        lax.fori_loop(0, PER // 2, pair, 0)
        if c == 0:
            pl.semaphore_wait(barrier, COLS + ROWS - 2)
        send_row(c)
        if c >= 1:
            row_totals(c - 1)
    load_kv.wait()
    for c in range(CHUNKS - 1):
        hidden(c)
        if c == 0:
            row_totals(CHUNKS - 1)
    hidden(CHUNKS - 1)
    kv[0, :HD] = kvacc[:, :HD].astype(BF16)
    kv[0, HD:] = kvacc[:, HD:].T.astype(BF16)

    halo = Halo(kv, halo_send, halo_recv, z, y)
    halo.each(halo.own)

    def attend(offsets):
        place, n = PLACE[offsets[0]], len(offsets)
        nk = n * HD
        first = offsets[0] == 0

        def qk(h, s):
            keys = kv[place : place + n, :HD].reshape(nk, HD)
            s[:nk] = lax.dot_general(
                keys, hid[h], (((1,), (1,)), ((), ())), preferred_element_type=F32
            )

        def soft(h, s, p, al):
            value = s[:nk]
            bias = bias0 if first else bias8 if offsets[0] == 8 else None
            if bias is not None:
                masked = value[:HD] + bias[...]
                value = masked if n == 1 else jnp.concatenate([masked, value[HD:]], axis=0)
            top = jnp.max(value, axis=0, keepdims=True)
            if not first:
                before = m[h]
                top = jnp.maximum(before, top)
                alpha = jnp.exp2((before - top) * SCALE2)
                al[...] = alpha
            m[h] = top
            e = jnp.exp2(value * SCALE2 - top * SCALE2)
            part = jnp.sum(e, axis=0, keepdims=True)
            l[h] = part if first else l[h] * alpha + part
            p[:nk] = e.astype(BF16)

        def pv(h, p, al):
            new = jnp.dot(kv[place, HD:], p[:HD], preferred_element_type=F32)
            if n == 2:
                new += jnp.dot(kv[place + 1, HD:], p[HD:], preferred_element_type=F32)
            acc[h] = new if first else acc[h] * al[...] + new

        qk(0, s_a)
        qk(1, s_b)
        soft(0, s_a, p_a, al_a)

        def body(i, _):
            h = 2 * i + 1
            qk(h + 1, s_a)
            pv(h - 1, p_a, al_a)
            soft(h, s_b, p_b, al_b)
            qk(h + 2, s_b)
            pv(h, p_b, al_b)
            soft(h + 1, s_a, p_a, al_a)
            return 0

        lax.fori_loop(0, HEADS // 2 - 1, body, 0)
        pv(HEADS - 2, p_a, al_a)
        soft(HEADS - 1, s_b, p_b, al_b)
        pv(HEADS - 1, p_b, al_b)

    attend((0,))
    halo.each(halo.first_row)
    for index, step in enumerate(STEPS):
        halo.need(step)

        @pl.when(me >= max(step))
        def _():
            attend(step)

        if len(step) == 2:
            @pl.when((me >= min(step)) & (me < max(step)))
            def _():
                attend((min(step),))

        if index == 0:
            halo.each(halo.second_row)
        if index == 1:
            halo.each(halo.last_row)

    back = permutation(True)
    perm[...] = back

    def finish(i, _):
        for u in range(2):
            h = 2 * i + u
            o = (acc[h] * (1.0 / l[h])).astype(BF16)
            out[:, lanes(h)] = lax.dot_general(
                perm[...], o, (((1,), (1,)), ((), ())), preferred_element_type=F32
            ).astype(BF16)
        return 0

    stores = []
    for c in range(CHUNKS):
        lax.fori_loop(c * PER // 2, (c + 1) * PER // 2, finish, 0)
        cols = pl.ds(c * PER * HD, PER * HD)
        store = pltpu.make_async_copy(out.at[:, cols], out_hbm.at[:, cols], out_sem.at[c])
        store.start()
        stores.append(store)

    halo.drain()
    for c in range(CHUNKS):
        for k in range(1, COLS):
            row_copy(c, k).wait_send()
        for to in range(1, ROWS):
            @pl.when(to > z)
            def _():
                col_copy(c, to).wait_send()
    for store in stores:
        store.wait()


def on_device(inputs, recur_weight, input_weight, recur_bias, input_bias, decay_rate, kv_weight):
    hbm = pl.BlockSpec(memory_space=pl.ANY)
    vmem = pl.BlockSpec(memory_space=pltpu.VMEM)
    tile = pltpu.VMEM((TOK, HD), F32)
    dma = pltpu.SemaphoreType.DMA
    return pl.pallas_call(
        kernel,
        in_specs=[hbm, hbm, hbm, vmem, vmem, vmem, hbm],
        out_specs=hbm,
        out_shape=jax.ShapeDtypeStruct((TOK, D), BF16),
        scratch_shapes=[
            pltpu.VMEM((TOK, D), BF16),
            pltpu.VMEM((HEADS, HD, HD), BF16),
            pltpu.VMEM((HEADS, HD, HD), BF16),
            pltpu.VMEM((HEADS, HD, 2 * HD), BF16),
            pltpu.VMEM((TOK, TOK), BF16),
            tile, tile, tile, tile, tile, tile,
            pltpu.VMEM((HEADS, TOK, HD), F32),
            pltpu.VMEM((HEADS, TOK, HD), F32),
            pltpu.VMEM((HEADS, 8, HD), F32),
            pltpu.VMEM((HEADS, 8, HD), F32),
            pltpu.VMEM((CHUNKS, COLS, 2, PER, 1, HD), F32),
            pltpu.VMEM((CHUNKS, 2, PER, 1, HD), F32),
            pltpu.VMEM((CHUNKS, ROWS, 2, PER, 1, HD), F32),
            pltpu.VMEM((PER, 1, HD), F32),
            pltpu.VMEM((HEADS, TOK, HD), BF16),
            pltpu.VMEM((TOK, 2 * HD), F32),
            pltpu.VMEM((9, 2 * HD, HD), BF16),
            tile, tile,
            pltpu.VMEM((HEADS, 1, TOK), F32),
            pltpu.VMEM((HEADS, 1, TOK), F32),
            pltpu.VMEM((HEADS, HD, TOK), F32),
            pltpu.VMEM((2 * HD, TOK), F32),
            pltpu.VMEM((2 * HD, TOK), F32),
            pltpu.VMEM((2 * HD, TOK), BF16),
            pltpu.VMEM((2 * HD, TOK), BF16),
            pltpu.VMEM((1, TOK), F32),
            pltpu.VMEM((1, TOK), F32),
            pltpu.VMEM((TOK, D), BF16),
            dma((3 * CHUNKS + 1,)),
            dma((CHUNKS, COLS - 1)),
            dma((CHUNKS, COLS)),
            dma((CHUNKS, ROWS)),
            dma((CHUNKS, ROWS)),
            dma((24,)),
            dma((9, 2)),
            dma((CHUNKS,)),
        ],
        compiler_params=pltpu.CompilerParams(
            collective_id=0, has_side_effects=True, vmem_limit_bytes=56 * 1024 * 1024
        ),
        name="layer",
    )(
        inputs, recur_weight, input_weight, recur_bias[None], input_bias[None],
        decay_rate[None], kv_weight.reshape(HEADS, HD, 2 * HD),
    )


def solution(mesh):
    placed = (P(("batch", "seq"), None), P(), P(), P(), P(), P(), P())
    return jax.shard_map(
        on_device, mesh=mesh, in_specs=placed, out_specs=P(("batch", "seq"), None), check_vma=False
    )
```

profile of v0, /device:TPU:68, one launch (start us, length us, event | category | flops | bytes accessed | tf_op | source)
XLA Modules:
  0.0 59.5 jit_solution(3674434999841454273)
XLA Ops:
  0.0 56.3 %layer.1 = bf16[256,4096]{1,0:T(8,128)(2,1)} custom-call(bf16[256,4096]{1,0:T(8,128)(2,1)} %x_hbm.1, bf16[16,256,256]{2,1,0:T(8,128)(2,1)} %wr_hbm.1, bf16[16,256,256]{2,1,0:T(8,128)(2,1)} %wi_hbm.1, f32[1,4096]{1,0:T(1,128)} %bitcast.5, f32[1,4096]{1,0:T(1,128)} %bitcast.6, f32[1,4096]{1,0:T(1,128)} %bitcast.7, bf16[16,256,512]{2,1,0:T(8,128)(2,1)} %bitcast.4), custom_call_target="tpu_custom_call" | custom-call | tf_op jit(solution)/shard_map/layer/pallas_call | solution.py:466
  56.3 3.1 %copy.9 = bf16[256,4096]{1,0:T(8,128)(2,1)} copy(bf16[256,4096]{1,0:T(8,128)(2,1)} %layer.1) | data formatting | bytes 4194304
where the time goes:
time: 59.7 us; the launch traced here: 59.5 us
  Pallas kernels  56.3 us (94%)
  local copies, waits for them, and re-layouts  3.13 us (5%)
    pallas_call x1, Pallas kernels, on_device(): pl.pallas_call(kernel, in_specs=[hbm, hbm, hbm, vmem, vmem, vmem, hbm], o...  56.3 us
    unnamed x1, local copies, waits for them, and re-layouts  3.13 us

commit v1 on v0

--- a/solution.py
+++ b/solution.py
@@ -168,11 +168,11 @@
 
 
 def kernel(
-    x_hbm, wr_hbm, wi_hbm, br, bi, rate, wkv_hbm, out_hbm,
-    x, wr, wi, wkv, perm, xp_a, lr_a, li_a, xp_b, lr_b, li_b, loc, cum, segc, segp,
+    x_hbm, wr_hbm, wi_hbm, br_hbm, bi_hbm, rate_hbm, wkv_hbm, out,
+    x, wr, wi, br, bi, rate, wkv, perm, xp_a, lr_a, li_a, xp_b, lr_b, li_b, loc, cum, segc, segp,
     rowtot, rowpre, coltot, carry, hid, kvacc, kv, bias0, bias8,
-    m, l, acc, s_a, s_b, p_a, p_b, al_a, al_b, out,
-    load_sem, row_send, row_recv, col_send, col_recv, halo_send, halo_recv, out_sem,
+    m, l, acc, s_a, s_b, p_a, p_b, al_a, al_b,
+    load_sem, row_send, row_recv, col_send, col_recv, halo_send, halo_recv,
 ):
     me = lax.axis_index("seq")
     z, y = me // COLS, me % COLS
@@ -186,6 +186,11 @@
             pltpu.make_async_copy(wi_hbm.at[blocks], wi.at[blocks], load_sem.at[3 * c + 2]),
         ])
     load_kv = pltpu.make_async_copy(wkv_hbm, wkv, load_sem.at[3 * CHUNKS])
+    small = [
+        pltpu.make_async_copy(src, dst, load_sem.at[3 * CHUNKS + 1 + k])
+        for k, (src, dst) in enumerate([(br_hbm, br), (bi_hbm, bi), (rate_hbm, rate)])
+    ]
+    loads[0] += small
     for group in loads:
         for load in group:
             load.start()
@@ -202,8 +207,8 @@
         )
 
     perm[...] = permutation(False)
-    kt = token_of(lax.broadcasted_iota(jnp.int32, (TOK, TOK), 0))
-    qt = token_of(lax.broadcasted_iota(jnp.int32, (TOK, TOK), 1))
+    kt = token_of(lax.broadcasted_iota(jnp.int32, (TOK, TOK), 1))
+    qt = token_of(lax.broadcasted_iota(jnp.int32, (TOK, TOK), 0))
     bias0[...] = jnp.where(kt <= qt, 0.0, NEG)
     bias8[...] = jnp.where(kt <= qt, NEG, 0.0)
 
@@ -339,114 +344,88 @@
         if c == 0:
             pl.semaphore_wait(barrier, COLS + ROWS - 2)
         send_row(c)
-        if c >= 1:
-            row_totals(c - 1)
+        if c >= 2:
+            row_totals(c - 2)
     load_kv.wait()
-    for c in range(CHUNKS - 1):
+    row_totals(CHUNKS - 2)
+    row_totals(CHUNKS - 1)
+    for c in range(CHUNKS):
         hidden(c)
-        if c == 0:
-            row_totals(CHUNKS - 1)
-    hidden(CHUNKS - 1)
     kv[0, :HD] = kvacc[:, :HD].astype(BF16)
-    kv[0, HD:] = kvacc[:, HD:].T.astype(BF16)
+    kv[0, HD:] = kvacc[:, HD:].astype(BF16)
 
     halo = Halo(kv, halo_send, halo_recv, z, y)
     halo.each(halo.own)
 
-    def attend(offsets):
+    def attend(offsets, group):
         place, n = PLACE[offsets[0]], len(offsets)
-        nk = n * HD
+        nk, count, height = n * HD, HEADS // group, group * TOK
         first = offsets[0] == 0
-
-        def qk(h, s):
+        bias = bias0 if first else bias8 if offsets[0] == 8 else None
+
+        def rows(g):
+            return pl.ds(pl.multiple_of(g * height, height), height)
+
+        def qk(g, s):
+            queries = hid[pl.ds(g * group, group)].reshape(height, HD)
             keys = kv[place : place + n, :HD].reshape(nk, HD)
-            s[:nk] = lax.dot_general(
-                keys, hid[h], (((1,), (1,)), ((), ())), preferred_element_type=F32
+            value = lax.dot_general(
+                queries, keys, (((1,), (1,)), ((), ())), preferred_element_type=F32
             )
-
-        def soft(h, s, p, al):
-            value = s[:nk]
-            bias = bias0 if first else bias8 if offsets[0] == 8 else None
             if bias is not None:
-                masked = value[:HD] + bias[...]
-                value = masked if n == 1 else jnp.concatenate([masked, value[HD:]], axis=0)
-            top = jnp.max(value, axis=0, keepdims=True)
+                masked = value[:, :HD].reshape(group, TOK, HD) + bias[...][None]
+                masked = masked.reshape(height, HD)
+                value = masked if n == 1 else jnp.concatenate([masked, value[:, HD:]], axis=1)
+            s[:height, :nk] = value
+
+        def soft(g, s, p, al):
+            value = s[:height, :nk]
+            r = rows(g)
+            top = jnp.broadcast_to(jnp.max(value, axis=1, keepdims=True), (height, 128))
             if not first:
-                before = m[h]
+                before = m[r]
                 top = jnp.maximum(before, top)
                 alpha = jnp.exp2((before - top) * SCALE2)
-                al[...] = alpha
-            m[h] = top
-            e = jnp.exp2(value * SCALE2 - top * SCALE2)
-            part = jnp.sum(e, axis=0, keepdims=True)
-            l[h] = part if first else l[h] * alpha + part
-            p[:nk] = e.astype(BF16)
-
-        def pv(h, p, al):
-            new = jnp.dot(kv[place, HD:], p[:HD], preferred_element_type=F32)
-            if n == 2:
-                new += jnp.dot(kv[place + 1, HD:], p[HD:], preferred_element_type=F32)
-            acc[h] = new if first else acc[h] * al[...] + new
+                al[:height] = alpha
+            m[r] = top
+            shift = top * SCALE2
+            part = None
+            for j in range(nk // 128):
+                e = jnp.exp2(value[:, 128 * j : 128 * j + 128] * SCALE2 - shift)
+                p[:height, 128 * j : 128 * j + 128] = e.astype(BF16)
+                part = e if part is None else part + e
+            l[r] = part if first else l[r] * alpha + part
+
+        def pv(g, p, al):
+            r = rows(g)
+            values = kv[place : place + n, HD:].reshape(nk, HD)
+            new = jnp.dot(p[:height, :nk], values, preferred_element_type=F32)
+            if first:
+                acc[r] = new
+            else:
+                alpha = al[:height]
+                acc[r] = acc[r] * jnp.concatenate([alpha, alpha], axis=1) + new
 
         qk(0, s_a)
         qk(1, s_b)
         soft(0, s_a, p_a, al_a)
 
         def body(i, _):
-            h = 2 * i + 1
-            qk(h + 1, s_a)
-            pv(h - 1, p_a, al_a)
-            soft(h, s_b, p_b, al_b)
-            qk(h + 2, s_b)
-            pv(h, p_b, al_b)
-            soft(h + 1, s_a, p_a, al_a)
+            g = 2 * i + 1
+            qk(g + 1, s_a)
+            pv(g - 1, p_a, al_a)
+            soft(g, s_b, p_b, al_b)
+            qk(g + 2, s_b)
+            pv(g, p_b, al_b)
+            soft(g + 1, s_a, p_a, al_a)
             return 0
 
-        lax.fori_loop(0, HEADS // 2 - 1, body, 0)
-        pv(HEADS - 2, p_a, al_a)
-        soft(HEADS - 1, s_b, p_b, al_b)
-        pv(HEADS - 1, p_b, al_b)
-
-    attend((0,))
-    halo.each(halo.first_row)
-    for index, step in enumerate(STEPS):
-        halo.need(step)
-
-        @pl.when(me >= max(step))
-        def _():
-            attend(step)
-
-        if len(step) == 2:
-            @pl.when((me >= min(step)) & (me < max(step)))
-            def _():
-                attend((min(step),))
-
-        if index == 0:
-            halo.each(halo.second_row)
-        if index == 1:
-            halo.each(halo.last_row)
-
-    back = permutation(True)
-    perm[...] = back
-
-    def finish(i, _):
-        for u in range(2):
-            h = 2 * i + u
-            o = (acc[h] * (1.0 / l[h])).astype(BF16)
-            out[:, lanes(h)] = lax.dot_general(
-                perm[...], o, (((1,), (1,)), ((), ())), preferred_element_type=F32
-            ).astype(BF16)
-        return 0
-
-    stores = []
-    for c in range(CHUNKS):
-        lax.fori_loop(c * PER // 2, (c + 1) * PER // 2, finish, 0)
-        cols = pl.ds(c * PER * HD, PER * HD)
-        store = pltpu.make_async_copy(out.at[:, cols], out_hbm.at[:, cols], out_sem.at[c])
-        store.start()
-        stores.append(store)
-
-    halo.drain()
+        lax.fori_loop(0, count // 2 - 1, body, 0)
+        pv(count - 2, p_a, al_a)
+        soft(count - 1, s_b, p_b, al_b)
+        pv(count - 1, p_b, al_b)
+
+    attend((0,), 4)
     for c in range(CHUNKS):
         for k in range(1, COLS):
             row_copy(c, k).wait_send()
@@ -454,24 +433,57 @@
             @pl.when(to > z)
             def _():
                 col_copy(c, to).wait_send()
-    for store in stores:
-        store.wait()
+
+    halo.each(halo.first_row)
+    for index, step in enumerate(STEPS):
+        halo.need(step)
+
+        @pl.when(me >= max(step))
+        def _():
+            attend(step, 4)
+
+        if len(step) == 2:
+            @pl.when((me >= min(step)) & (me < max(step)))
+            def _():
+                attend((min(step),), 1)
+
+        if index == 0:
+            halo.each(halo.second_row)
+        if index == 1:
+            halo.each(halo.last_row)
+
+    perm[...] = permutation(True)
+
+    def finish(i, _):
+        for u in range(PER):
+            h = PER * i + u
+            r = pl.ds(pl.multiple_of(h * TOK, TOK), TOK)
+            total = jnp.sum(l[r], axis=1, keepdims=True)
+            o = (acc[r] * (1.0 / total)).astype(BF16)
+            out[:, lanes(h)] = jnp.dot(perm[...], o, preferred_element_type=F32).astype(BF16)
+        return 0
+
+    lax.fori_loop(0, CHUNKS, finish, 0)
+    halo.drain()
 
 
 def on_device(inputs, recur_weight, input_weight, recur_bias, input_bias, decay_rate, kv_weight):
-    hbm = pl.BlockSpec(memory_space=pl.ANY)
+    hbm = pl.BlockSpec(memory_space=pltpu.HBM)
     vmem = pl.BlockSpec(memory_space=pltpu.VMEM)
     tile = pltpu.VMEM((TOK, HD), F32)
     dma = pltpu.SemaphoreType.DMA
     return pl.pallas_call(
         kernel,
-        in_specs=[hbm, hbm, hbm, vmem, vmem, vmem, hbm],
-        out_specs=hbm,
+        in_specs=[hbm] * 7,
+        out_specs=vmem,
         out_shape=jax.ShapeDtypeStruct((TOK, D), BF16),
         scratch_shapes=[
             pltpu.VMEM((TOK, D), BF16),
             pltpu.VMEM((HEADS, HD, HD), BF16),
             pltpu.VMEM((HEADS, HD, HD), BF16),
+            pltpu.VMEM((1, D), F32),
+            pltpu.VMEM((1, D), F32),
+            pltpu.VMEM((1, D), F32),
             pltpu.VMEM((HEADS, HD, 2 * HD), BF16),
             pltpu.VMEM((TOK, TOK), BF16),
             tile, tile, tile, tile, tile, tile,
@@ -487,27 +499,25 @@
             pltpu.VMEM((TOK, 2 * HD), F32),
             pltpu.VMEM((9, 2 * HD, HD), BF16),
             tile, tile,
-            pltpu.VMEM((HEADS, 1, TOK), F32),
-            pltpu.VMEM((HEADS, 1, TOK), F32),
-            pltpu.VMEM((HEADS, HD, TOK), F32),
-            pltpu.VMEM((2 * HD, TOK), F32),
-            pltpu.VMEM((2 * HD, TOK), F32),
-            pltpu.VMEM((2 * HD, TOK), BF16),
-            pltpu.VMEM((2 * HD, TOK), BF16),
-            pltpu.VMEM((1, TOK), F32),
-            pltpu.VMEM((1, TOK), F32),
-            pltpu.VMEM((TOK, D), BF16),
-            dma((3 * CHUNKS + 1,)),
+            pltpu.VMEM((HEADS * TOK, 128), F32),
+            pltpu.VMEM((HEADS * TOK, 128), F32),
+            pltpu.VMEM((HEADS * TOK, HD), F32),
+            pltpu.VMEM((4 * TOK, 2 * HD), F32),
+            pltpu.VMEM((4 * TOK, 2 * HD), F32),
+            pltpu.VMEM((4 * TOK, 2 * HD), BF16),
+            pltpu.VMEM((4 * TOK, 2 * HD), BF16),
+            pltpu.VMEM((4 * TOK, 128), F32),
+            pltpu.VMEM((4 * TOK, 128), F32),
+            dma((3 * CHUNKS + 4,)),
             dma((CHUNKS, COLS - 1)),
             dma((CHUNKS, COLS)),
             dma((CHUNKS, ROWS)),
             dma((CHUNKS, ROWS)),
             dma((24,)),
             dma((9, 2)),
-            dma((CHUNKS,)),
         ],
         compiler_params=pltpu.CompilerParams(
-            collective_id=0, has_side_effects=True, vmem_limit_bytes=56 * 1024 * 1024
+            collective_id=0, has_side_effects=True, vmem_limit_bytes=51 * 1024 * 1024
         ),
         name="layer",
     )(

time: 59.7 us -> 54.8 us (0.918)
  the two profiles are of different devices: /device:TPU:68 before, /device:TPU:230 now
where the time goes in v1:
time: 54.8 us; the launch traced here: 54.5 us
  Pallas kernels  51 us (93%)
  local copies, waits for them, and re-layouts  3.47 us (6%)
    pallas_call x1, Pallas kernels, on_device(): pl.pallas_call(kernel, in_specs=[hbm] * 7, out_specs=vmem, out_shape=jax....  51 us
    unnamed x7, local copies, waits for them, and re-layouts  3.47 us

profile of v1, /device:TPU:230, one launch (start us, length us, event | category | flops | bytes accessed | tf_op | source)
XLA Modules:
  0.0 54.5 jit_solution(1186299813135620159)
XLA Ops:
  0.0 0.0 copy-start
  0.0 0.7 %copy-done = f32[4096]{0:T(1024)S(1)} copy-done((f32[4096]{0:T(1024)S(1)}, f32[4096]{0:T(1024)}, u32[]{:S(2)}) %copy-start) | copy-done | bytes 16408
  0.7 0.0 copy-start.1
  0.7 0.7 %copy-done.1 = f32[4096]{0:T(1024)S(1)} copy-done((f32[4096]{0:T(1024)S(1)}, f32[4096]{0:T(1024)}, u32[]{:S(2)}) %copy-start.1) | copy-done | bytes 16408
  1.4 0.0 copy-start.2
  1.4 0.7 %copy-done.2 = f32[4096]{0:T(1024)S(1)} copy-done((f32[4096]{0:T(1024)S(1)}, f32[4096]{0:T(1024)}, u32[]{:S(2)}) %copy-start.2) | copy-done | bytes 16408
  2.2 51.0 %layer.1 = bf16[256,4096]{1,0:T(8,128)(2,1)S(1)} custom-call(bf16[256,4096]{1,0:T(8,128)(2,1)} %x_hbm.1, bf16[16,256,256]{2,1,0:T(8,128)(2,1)} %wr_hbm.1, bf16[16,256,256]{2,1,0:T(8,128)(2,1)} %wi_hbm.1, f32[1,4096]{1,0:T(1,128)S(1)} %bitcast.4, f32[1,4096]{1,0:T(1,128)S(1)} %bitcast.5, f32[1,4096]{1,0:T(1,128)S(1)} %bitcast.6, bf16[16,256,512]{2,1,0:T(8,128)(2,1)} %bitcast.7), custom_call_target="tpu_custom_call" | custom-call | tf_op jit(solution)/shard_map/layer/pallas_call | solution.py:475
  53.1 1.3 %copy.9 = bf16[256,4096]{1,0:T(8,128)(2,1)} copy(bf16[256,4096]{1,0:T(8,128)(2,1)S(1)} %layer.1) | data formatting | bytes 4194304
Async XLA Ops:
  0.0 0.7 %copy-start = (f32[4096]{0:T(1024)S(1)}, f32[4096]{0:T(1024)}, u32[]{:S(2)}) copy-start(f32[4096]{0:T(1024)} %param.10) | copy-start | bytes 49156
  0.7 0.7 %copy-start.1 = (f32[4096]{0:T(1024)S(1)}, f32[4096]{0:T(1024)}, u32[]{:S(2)}) copy-start(f32[4096]{0:T(1024)} %param.11) | copy-start | bytes 49156
  1.4 0.7 %copy-start.2 = (f32[4096]{0:T(1024)S(1)}, f32[4096]{0:T(1024)}, u32[]{:S(2)}) copy-start(f32[4096]{0:T(1024)} %param.12) | copy-start | bytes 49156

commit v2 on v1

--- a/solution.py
+++ b/solution.py
@@ -15,6 +15,9 @@
 COLS = 4
 CHUNKS = 4
 PER = HEADS // CHUNKS
+PARTS = 4
+KEYS = range(PARTS // 2)
+VALUES = range(PARTS // 2, PARTS)
 LOG2E = math.log2(math.e)
 SCALE2 = (HD ** -0.5) * LOG2E
 NEG = -1e30
@@ -51,7 +54,8 @@
         self.started = [[] for _ in range(COLS)]
 
     def half(self, o, part):
-        return self.kv.at[PLACE[o], pl.ds(part * HD, HD)]
+        size = 2 * HD // PARTS
+        return self.kv.at[PLACE[o], pl.ds(part * size, size)]
 
     def copy(self, index, src, dst, part, dz, dst_y):
         return pltpu.make_async_remote_copy(
@@ -100,7 +104,7 @@
                 fn(yy)
 
     def own(self, yy):
-        for part in (0, 1):
+        for part in range(PARTS):
             self.start(yy, 0, part, 1, yy)
             if yy < COLS - 1:
                 self.start(yy, 0, part, 0, yy + 1)
@@ -108,51 +112,55 @@
                 self.start(yy, 0, part, 0, COLS - 1)
 
     def first_row(self, yy):
-        for part in (0, 1):
+        for part in range(PARTS):
             self.arrive(yy, 4, part)
             self.start(yy, 4, part, 1, yy)
             self.start(yy, 4, part, 0, (yy + 1) % COLS)
             self.start(yy, 4, part, 0, (yy - 1) % COLS)
-            if yy == 1 and part == 0:
-                self.arrive(yy, 1, 0)
-                self.start(yy, 1, 0, 0, 2)
+            if yy == 1 and part in KEYS:
+                self.arrive(yy, 1, part)
+                self.start(yy, 1, part, 0, 2)
             if yy == 2:
                 self.arrive(yy, 1, part)
                 self.start(yy, 1, part, 0, 3)
-            if yy == 3 and part == 1:
-                self.arrive(yy, 3, 1)
-                self.start(yy, 3, 1, 0, 2)
+            if yy == 3 and part in VALUES:
+                self.arrive(yy, 3, part)
+                self.start(yy, 3, part, 0, 2)
 
     def second_row(self, yy):
         left, right = (yy - 1) % COLS, (yy + 1) % COLS
         from_left, from_right = 4 + yy - left, 4 + yy - right
-        self.arrive(yy, from_left, 0)
-        self.start(yy, from_left, 0, 0, right)
-        for part in (0, 1):
+        for part in range(PARTS):
             self.arrive(yy, 8, part)
             if yy >= 1:
                 self.start(yy, 8, part, 0, yy - 1)
             if yy == COLS - 1:
                 self.start(yy, 8, part, 0, 0)
-        self.arrive(yy, from_right, 1)
-        self.start(yy, from_right, 1, 0, left)
+            if part in KEYS:
+                self.arrive(yy, from_left, part)
+                self.start(yy, from_left, part, 0, right)
+            else:
+                self.arrive(yy, from_right, part)
+                self.start(yy, from_right, part, 0, left)
 
     def last_row(self, yy):
         if yy == 0:
-            self.arrive(yy, 5, 1)
-            self.start(yy, 5, 1, 0, 1)
+            for part in VALUES:
+                self.arrive(yy, 5, part)
+                self.start(yy, 5, part, 0, 1)
         if yy == 1:
-            for part in (0, 1):
+            for part in range(PARTS):
                 self.arrive(yy, 7, part)
                 self.start(yy, 7, part, 0, 0)
         if yy == 2:
-            self.arrive(yy, 7, 0)
-            self.start(yy, 7, 0, 0, 1)
+            for part in KEYS:
+                self.arrive(yy, 7, part)
+                self.start(yy, 7, part, 0, 1)
 
     def need(self, step):
         def fn(yy):
             for o in step:
-                for part in (0, 1):
+                for part in range(PARTS):
                     self.arrive(yy, o, part)
 
         self.each(fn)
@@ -169,7 +177,7 @@
 
 def kernel(
     x_hbm, wr_hbm, wi_hbm, br_hbm, bi_hbm, rate_hbm, wkv_hbm, out,
-    x, wr, wi, br, bi, rate, wkv, perm, xp_a, lr_a, li_a, xp_b, lr_b, li_b, loc, cum, segc, segp,
+    x, wr, wi, br, bi, rate, wkv, perm, back, xp_a, lr_a, li_a, xp_b, lr_b, li_b, loc, cum, segc, segp,
     rowtot, rowpre, coltot, carry, hid, kvacc, kv, bias0, bias8,
     m, l, acc, s_a, s_b, p_a, p_b, al_a, al_b,
     load_sem, row_send, row_recv, col_send, col_recv, halo_send, halo_recv,
@@ -207,6 +215,7 @@
         )
 
     perm[...] = permutation(False)
+    back[...] = permutation(True)
     kt = token_of(lax.broadcasted_iota(jnp.int32, (TOK, TOK), 1))
     qt = token_of(lax.broadcasted_iota(jnp.int32, (TOK, TOK), 0))
     bias0[...] = jnp.where(kt <= qt, 0.0, NEG)
@@ -340,7 +349,8 @@
             scan(b + 1, c, xp_b, lr_b, li_b)
             return 0
 
-        lax.fori_loop(0, PER // 2, pair, 0)
+        for i in range(PER // 2):
+            pair(i, 0)
         if c == 0:
             pl.semaphore_wait(barrier, COLS + ROWS - 2)
         send_row(c)
@@ -357,7 +367,12 @@
     halo = Halo(kv, halo_send, halo_recv, z, y)
     halo.each(halo.own)
 
-    def attend(offsets, group):
+    def finish(h, weighted, total):
+        total = jnp.sum(total, axis=1, keepdims=True)
+        o = (weighted * (1.0 / total)).astype(BF16)
+        out[:, lanes(h)] = jnp.dot(back[...], o, preferred_element_type=F32).astype(BF16)
+
+    def attend(offsets, group, final=False):
         place, n = PLACE[offsets[0]], len(offsets)
         nk, count, height = n * HD, HEADS // group, group * TOK
         first = offsets[0] == 0
@@ -404,7 +419,14 @@
                 acc[r] = new
             else:
                 alpha = al[:height]
-                acc[r] = acc[r] * jnp.concatenate([alpha, alpha], axis=1) + new
+                new = acc[r] * jnp.concatenate([alpha, alpha], axis=1) + new
+                if not final:
+                    acc[r] = new
+                    return
+                total = l[r]
+                for u in range(group):
+                    part = slice(u * TOK, u * TOK + TOK)
+                    finish(g * group + u, new[part], total[part])
 
         qk(0, s_a)
         qk(1, s_b)
@@ -440,7 +462,7 @@
 
         @pl.when(me >= max(step))
         def _():
-            attend(step, 4)
+            attend(step, 4, final=index == len(STEPS) - 1)
 
         if len(step) == 2:
             @pl.when((me >= min(step)) & (me < max(step)))
@@ -452,19 +474,22 @@
         if index == 1:
             halo.each(halo.last_row)
 
-    perm[...] = permutation(True)
-
-    def finish(i, _):
+    def finish_four(i, _):
         for u in range(PER):
             h = PER * i + u
             r = pl.ds(pl.multiple_of(h * TOK, TOK), TOK)
-            total = jnp.sum(l[r], axis=1, keepdims=True)
-            o = (acc[r] * (1.0 / total)).astype(BF16)
-            out[:, lanes(h)] = jnp.dot(perm[...], o, preferred_element_type=F32).astype(BF16)
+            finish(h, acc[r], l[r])
         return 0
 
-    lax.fori_loop(0, CHUNKS, finish, 0)
+    @pl.when(me < STEPS[-1][0])
+    def _():
+        lax.fori_loop(0, CHUNKS, finish_four, 0)
+
     halo.drain()
+
+
+def keep(v):
+    return pltpu.with_memory_space_constraint(v, pltpu.HBM)
 
 
 def on_device(inputs, recur_weight, input_weight, recur_bias, input_bias, decay_rate, kv_weight):
@@ -485,6 +510,7 @@
             pltpu.VMEM((1, D), F32),
             pltpu.VMEM((1, D), F32),
             pltpu.VMEM((HEADS, HD, 2 * HD), BF16),
+            pltpu.VMEM((TOK, TOK), BF16),
             pltpu.VMEM((TOK, TOK), BF16),
             tile, tile, tile, tile, tile, tile,
             pltpu.VMEM((HEADS, TOK, HD), F32),
@@ -513,16 +539,16 @@
             dma((CHUNKS, COLS)),
             dma((CHUNKS, ROWS)),
             dma((CHUNKS, ROWS)),
-            dma((24,)),
-            dma((9, 2)),
+            dma((17 * PARTS // 2,)),
+            dma((9, PARTS)),
         ],
         compiler_params=pltpu.CompilerParams(
             collective_id=0, has_side_effects=True, vmem_limit_bytes=51 * 1024 * 1024
         ),
         name="layer",
     )(
-        inputs, recur_weight, input_weight, recur_bias[None], input_bias[None],
-        decay_rate[None], kv_weight.reshape(HEADS, HD, 2 * HD),
+        inputs, recur_weight, input_weight, keep(recur_bias[None]), keep(input_bias[None]),
+        keep(decay_rate[None]), kv_weight.reshape(HEADS, HD, 2 * HD),
     )
 
 

time: 54.8 us -> 50.7 us (0.925)
  local copies, waits for them, and re-layouts: 3.47 us -> 1.32 us
  Pallas kernels: 51 us -> 49 us
    unnamed x7 -> x1, local copies, waits for them, and re-layouts: 3.47 us -> 1.32 us
    pallas_call x1, Pallas kernels: 51 us -> 49 us  [on_device(): pl.pallas_call(kernel, in_specs=[hbm] * 7, out_specs=vmem, out_shape=jax....]
where the time goes in v2:
time: 50.7 us; the launch traced here: 50.4 us
  Pallas kernels  49 us (97%)
  local copies, waits for them, and re-layouts  1.32 us (3%)
    pallas_call x1, Pallas kernels, on_device(): pl.pallas_call(kernel, in_specs=[hbm] * 7, out_specs=vmem, out_shape=jax....  49 us
    unnamed x1, local copies, waits for them, and re-layouts  1.32 us

profile of v2, /device:TPU:230, one launch (start us, length us, event | category | flops | bytes accessed | tf_op | source)
XLA Modules:
  0.0 50.4 jit_solution(16682823990235962418)
XLA Ops:
  0.0 49.0 %layer.1 = bf16[256,4096]{1,0:T(8,128)(2,1)S(1)} custom-call(bf16[256,4096]{1,0:T(8,128)(2,1)} %x_hbm.1, bf16[16,256,256]{2,1,0:T(8,128)(2,1)} %wr_hbm.1, bf16[16,256,256]{2,1,0:T(8,128)(2,1)} %wi_hbm.1, f32[1,4096]{1,0:T(1,128)} %bitcast.5, f32[1,4096]{1,0:T(1,128)} %bitcast.6, f32[1,4096]{1,0:T(1,128)} %bitcast.7, bf16[16,256,512]{2,1,0:T(8,128)(2,1)} %bitcast.4), custom_call_target="tpu_custom_call" | custom-call | tf_op jit(solution)/shard_map/layer/pallas_call | solution.py:500
  49.0 1.3 %copy.9 = bf16[256,4096]{1,0:T(8,128)(2,1)} copy(bf16[256,4096]{1,0:T(8,128)(2,1)S(1)} %layer.1) | data formatting | bytes 4194304

commit v3 on v2

--- a/solution.py
+++ b/solution.py
@@ -117,6 +117,11 @@
             self.start(yy, 4, part, 1, yy)
             self.start(yy, 4, part, 0, (yy + 1) % COLS)
             self.start(yy, 4, part, 0, (yy - 1) % COLS)
+
+    def second_row(self, yy):
+        left, right = (yy - 1) % COLS, (yy + 1) % COLS
+        from_left, from_right = 4 + yy - left, 4 + yy - right
+        for part in range(PARTS):
             if yy == 1 and part in KEYS:
                 self.arrive(yy, 1, part)
                 self.start(yy, 1, part, 0, 2)
@@ -126,10 +131,6 @@
             if yy == 3 and part in VALUES:
                 self.arrive(yy, 3, part)
                 self.start(yy, 3, part, 0, 2)
-
-    def second_row(self, yy):
-        left, right = (yy - 1) % COLS, (yy + 1) % COLS
-        from_left, from_right = 4 + yy - left, 4 + yy - right
         for part in range(PARTS):
             self.arrive(yy, 8, part)
             if yy >= 1:

time: 50.7 us -> 50.1 us (0.988)
  no operation moved by 1% of the time
where the time goes in v3:
time: 50.1 us
  Pallas kernels  48.7 us (97%)
  local copies, waits for them, and re-layouts  1.32 us (3%)
    pallas_call x1, Pallas kernels, on_device(): pl.pallas_call(kernel, in_specs=[hbm] * 7, out_specs=vmem, out_shape=jax....  48.7 us
    unnamed x1, local copies, waits for them, and re-layouts  1.32 us

profile of v3, /device:TPU:230, one launch (start us, length us, event | category | flops | bytes accessed | tf_op | source)
XLA Modules:
  0.0 50.1 jit_solution(16089695146184160445)
XLA Ops:
  0.0 48.7 %layer.1 = bf16[256,4096]{1,0:T(8,128)(2,1)S(1)} custom-call(bf16[256,4096]{1,0:T(8,128)(2,1)} %x_hbm.1, bf16[16,256,256]{2,1,0:T(8,128)(2,1)} %wr_hbm.1, bf16[16,256,256]{2,1,0:T(8,128)(2,1)} %wi_hbm.1, f32[1,4096]{1,0:T(1,128)} %bitcast.5, f32[1,4096]{1,0:T(1,128)} %bitcast.6, f32[1,4096]{1,0:T(1,128)} %bitcast.7, bf16[16,256,512]{2,1,0:T(8,128)(2,1)} %bitcast.4), custom_call_target="tpu_custom_call" | custom-call | tf_op jit(solution)/shard_map/layer/pallas_call | solution.py:501
  48.7 1.3 %copy.9 = bf16[256,4096]{1,0:T(8,128)(2,1)} copy(bf16[256,4096]{1,0:T(8,128)(2,1)S(1)} %layer.1) | data formatting | bytes 4194304
